TPU v7x, 256 devices: a whole 4x4x8 slice. The times are simulated.
256 devices in a mesh: dp: 16 (over x, z_lo), hyper: 16 (over y, z_hi, core).
Axes of the slice: x: 4, y: 4, z: 8 (z_hi: 2, z_lo: 4; z = z_hi * 4 + z_lo), core: 2. Of those that a mesh axis runs over, the one named last changes fastest.
Arguments:
- inputs: bfloat16 [512, 64, 128], P(('dp', 'hyper')), may hold values from -64 to 64
- labels: int32 [512, 64], P(('dp', 'hyper')), may hold values from 0 to 255
- client_ids: int32 [512], P(('dp', 'hyper')), may hold values from 0 to 511
- ext_weight: bfloat16 [128, 4096], replicated, may hold values from -0.5 to 0.5
- ext_bias: bfloat16 [4096], replicated, may hold values from -3 to 3
- embeddings: bfloat16 [512, 128], replicated, may hold values from -1.5 to 1.5
- hyper_in: bfloat16 [128, 50], replicated, may hold values from -2.09375 to 2.09375
- hyper_bias: float32 [50], replicated, may hold values from -3 to 3
- hyper_out: bfloat16 [4096, 50, 256], P('hyper'), may hold values from -0.1796875 to 0.1796875
Outputs:
- grad_ext_weight: float32 [128, 4096], replicated
- grad_ext_bias: float32 [4096], replicated
- grad_embeddings: float32 [512, 128], replicated
- grad_hyper_in: float32 [128, 50], replicated
- grad_hyper_bias: float32 [50], replicated
- grad_hyper_out: float32 [4096, 50, 256], P(('hyper', 'dp'))
Inputs may be any that keep to these rules, and one draw needn't show every extreme that they name: `client_ids`: A client may hold several slots or none.
All inputs are finite; a program needn't handle non-finite values.
Results may differ from a plain program's by a relative error of at most 0.014.
The roundings to bfloat16 on the way count: a program that leaves them out, or rounds other values in their place, can miss the bound.
Values may be sent and summed in bfloat16 or wider, within the bound.
A program may use at most 128 MiB of HBM per device.

v0:
```python
import jax
import jax.numpy as jnp
from jax import lax
from jax.sharding import Mesh
from jax.sharding import PartitionSpec as P

DP = ("dp_0", "dp_1")
DP_HYPER = ("dp_0", "dp_1", "hyper")
HYPER_DP = ("hyper", "dp_0", "dp_1")


def sent_to_all(value, axis):
    copies = jnp.broadcast_to(value, (lax.axis_size(axis), *value.shape))
    return lax.all_to_all(copies, axis, split_axis=0, concat_axis=0, tiled=True)


def laid_out(tiles, dim):
    lengths = list(tiles.shape[1:])
    lengths[dim] *= tiles.shape[0]
    return jnp.moveaxis(tiles, 0, dim).reshape(lengths)


def gather_directly(value, axis, dim):
    tiles = sent_to_all(value, axis)
    return laid_out(tiles, dim)


def own_rows(terms, axes):
    total = terms.astype(jnp.bfloat16)
    for axis in axes:
        total = lax.psum_scatter(total, axis, scatter_dimension=0, tiled=True)
    return total.astype(jnp.float32)


def silu_slope(values):
    logistic = jax.nn.sigmoid(values)
    return logistic * (1.0 + values * (1.0 - logistic))


def class_grads(logits, slot_labels, row_count):
    largest = jnp.max(logits, axis=-1, keepdims=True)
    exponent = jnp.exp(logits - largest)
    probability = exponent / jnp.sum(exponent, axis=-1, keepdims=True)
    classes = jnp.arange(logits.shape[-1], dtype=jnp.int32)
    onehot = (slot_labels[..., None] == classes).astype(jnp.float32)
    return ((probability - onehot) / row_count).astype(jnp.bfloat16)


def local(
    inputs, labels, client_ids, ext_weight, ext_bias, embeddings, hyper_in, hyper_bias, hyper_out
):
    slot_count, row_count, width_in = inputs.shape
    width = ext_weight.shape[1]
    flat_in = inputs.reshape(slot_count * row_count, width_in)
    preact = jnp.dot(flat_in, ext_weight, preferred_element_type=jnp.float32) + ext_bias.astype(
        jnp.float32
    )
    features = jax.nn.silu(preact).astype(jnp.bfloat16).reshape(slot_count, row_count, width)
    row_ids = gather_directly(client_ids, "hyper", 0)
    table_ids = jnp.arange(embeddings.shape[0], dtype=jnp.int32)
    select = (row_ids[:, None] == table_ids[None, :]).astype(jnp.bfloat16)
    picked = jnp.dot(select, embeddings, preferred_element_type=jnp.float32).astype(jnp.bfloat16)
    hyper_preact = jnp.dot(picked, hyper_in, preferred_element_type=jnp.float32) + hyper_bias
    hidden = jax.nn.silu(hyper_preact).astype(jnp.bfloat16)
    head_part = jnp.einsum(
        "kh,dhc->kdc", hidden, hyper_out, preferred_element_type=jnp.float32
    ).astype(jnp.bfloat16)
    feat_cols = lax.all_to_all(features, "hyper", split_axis=2, concat_axis=0, tiled=True)
    logits = lax.psum_scatter(
        jnp.einsum("krd,kdc->krc", feat_cols, head_part, preferred_element_type=jnp.float32),
        "hyper",
        scatter_dimension=0,
        tiled=True,
    )
    dlogits = class_grads(logits, labels, row_count)
    dlog_rows = lax.all_gather(dlogits, "hyper", axis=0, tiled=True)
    dhead_part = jnp.einsum(
        "krd,krc->kdc", feat_cols, dlog_rows, preferred_element_type=jnp.float32
    ).astype(jnp.bfloat16)
    dfeat_cols = jnp.einsum(
        "krc,kdc->krd", dlog_rows, head_part, preferred_element_type=jnp.float32
    ).astype(jnp.bfloat16)
    dfeatures = lax.all_to_all(dfeat_cols, "hyper", split_axis=0, concat_axis=2, tiled=True)
    dpreact = (
        dfeatures.reshape(slot_count * row_count, width).astype(jnp.float32) * silu_slope(preact)
    ).astype(jnp.bfloat16)
    grad_weight = jnp.dot(flat_in.T, dpreact, preferred_element_type=jnp.float32)
    grad_bias = jnp.sum(dpreact.astype(jnp.float32), axis=0)
    grad_out = own_rows(
        jnp.einsum("kh,kdc->dhc", hidden, dhead_part, preferred_element_type=jnp.float32), DP
    )
    dhidden = jnp.einsum("kdc,dhc->kh", dhead_part, hyper_out, preferred_element_type=jnp.float32)
    hyper_dpre = dhidden * silu_slope(hyper_preact)
    grad_in = jnp.dot(picked.astype(jnp.float32).T, hyper_dpre)
    grad_hbias = jnp.sum(hyper_dpre, axis=0)
    back_rows = jnp.dot(hyper_dpre, hyper_in.astype(jnp.float32).T)
    grad_table = jnp.dot(select.astype(jnp.float32).T, back_rows)
    grad_weight, grad_bias, grad_table, grad_in, grad_hbias = lax.psum(
        (grad_weight, grad_bias, grad_table, grad_in, grad_hbias), DP_HYPER
    )
    return (grad_weight, grad_bias, grad_table, grad_in, grad_hbias, grad_out)


def solution(mesh):
    torus = Mesh(mesh.devices.reshape(4, 4, mesh.shape["hyper"]), ("dp_0", "dp_1", "hyper"))
    placed = (
        P(DP_HYPER, None, None),
        P(DP_HYPER, None),
        P(DP_HYPER),
        P(),
        P(),
        P(),
        P(),
        P(),
        P("hyper", None, None),
    )
    return jax.shard_map(
        local,
        mesh=torus,
        in_specs=placed,
        out_specs=(P(), P(), P(), P(), P(), P(HYPER_DP, None, None)),
        check_vma=False,
    )
```

profile of v0, /device:TPU:6, one launch (start us, length us, event | category | flops | bytes accessed | tf_op | source)
XLA Modules:
  0.0 629.3 jit_solution(14461696702569586145)
XLA Ops:
  8.5 11.2 %all-to-all-start.1 = ((s32[16,1,2]{2,1,0:T(1,128)}), s32[16,1,2]{2,1,0:T(1,128)S(1)}, u32[]{:S(2)}, u32[]{:S(2)}) async-start(s32[16,1,2]{2,1,0:T(1,128)} %broadcast_in_dim.2), calls=%async_computation.1 | async-start | bytes 16384 | tf_op jit(solution)/shard_map/all_to_all | solution.py:14
  20.4 3.1 multiply_convert_fusion.1
  23.5 5.0 copy.35
  28.6 2.2 reshape.50
  30.9 9.6 %all-to-all-start = ((bf16[16,2,16384]{2,1,0:T(2,128)(2,1)}), bf16[16,2,16384]{2,1,0:T(2,128)(2,1)S(1)}, u32[]{:S(2)}, u32[]{:S(2)}) async-start(bf16[16,2,16384]{2,1,0:T(2,128)(2,1)} %reshape.50), calls=%async_computation | async-start | bytes 2097152 | tf_op jit(solution)/shard_map/all_to_all | solution.py:68
  42.2 10.5 %fusion.9 = bf16[32,256,256]{2,0,1:T(8,128)(2,1)} fusion(bf16[256,50,256]{2,0,1:T(8,128)(2,1)} %param.17, f32[32,50]{1,0:T(8,128)S(1)} %convolution_add_fusion.1), kind=kOutput, calls=%fused_computation.12 | convolution fusion | flops 211820352 | bytes 10754304 | tf_op jit(solution)/shard_map/kh,dhc->kdc/dot_general | solution.py:65
  52.7 10.5 %all-to-all-done = bf16[16,2,16384]{2,1,0:T(2,128)(2,1)S(1)} async-done(((bf16[16,2,16384]{2,1,0:T(2,128)(2,1)}), bf16[16,2,16384]{2,1,0:T(2,128)(2,1)S(1)}, u32[]{:S(2)}, u32[]{:S(2)}) %all-to-all-start) | async-done | bytes 1048608 | tf_op jit(solution)/shard_map/all_to_all | solution.py:68
  63.2 2.4 reshape.51
  65.6 4.5 copy.36
  70.1 6.0 fusion.7
  76.1 91.6 %reduce-scatter.4.cloned.1.call-done = f32[2,64,256]{2,1,0:T(8,128)} async-done(((f32[32,64,256]{2,1,0:T(8,128)}), f32[2,64,256]{2,1,0:T(8,128)}) %reduce-scatter.4.cloned.1.call-update) | async-done | bytes 131088 | tf_op jit(solution)/shard_map/reduce_scatter | solution.py:69
  169.8 52.8 %all-gather.2.cloned.1.call-done = bf16[32,64,256]{2,1,0:T(8,128)(2,1)} async-done(((bf16[2,64,256]{2,1,0:T(8,128)(2,1)}), bf16[32,64,256]{2,1,0:T(8,128)(2,1)}) %all-gather.2.cloned.1.call-update) | async-done | bytes 1048592 | tf_op jit(solution)/shard_map/all_gather | solution.py:76
  222.6 2.5 convolution_convert_fusion
  227.1 6.0 convert_bitcast_fusion
  234.3 5.7 fusion.12
  240.1 3.8 all-to-all-start.2
  244.1 11.3 %copy.42 = bf16[256,50,256]{0,1,2:T(8,128)(2,1)} copy(bf16[256,50,256]{2,0,1:T(8,128)(2,1)} %param.17) | data formatting | bytes 13107200 | tf_op args[8]
  255.5 7.9 %copy.41 = bf16[32,256,256]{1,0,2:T(8,128)(2,1)} copy(bf16[32,256,256]{2,1,0:T(8,128)(2,1)} %copy-done.1) | data formatting | bytes 8388608 | tf_op jit(solution)/shard_map/convert_element_type | solution.py:79
  263.4 6.5 %fusion.30 = (f32[50]{0:T(128)S(1)}, bf16[32,50]{1,0:T(8,128)(2,1)S(1)}) fusion(f32[32,50]{1,0:T(8,128)S(1)} %convolution_add_fusion.1, bf16[32,256,256]{1,0,2:T(8,128)(2,1)} %copy.41, bf16[256,50,256]{0,1,2:T(8,128)(2,1)} %copy.42), kind=kOutput, calls=%fused_computation.40 | convolution fusion | flops 209731152 | bytes 10757704 | tf_op jit(solution)/shard_map/kdc,dhc->kh/dot_general | solution.py:92
  276.0 26.1 %reduce-scatter.6.cloned.1.call-done = bf16[64,50,256]{2,1,0:T(8,128)(2,1)} async-done(((bf16[256,50,256]{2,1,0:T(8,128)(2,1)}), bf16[64,50,256]{2,1,0:T(8,128)(2,1)}) %reduce-scatter.6.cloned.1.call-update) | async-done | bytes 1638416 | tf_op jit(solution)/shard_map/reduce_scatter | solution.py:31
  302.3 78.2 %all-reduce = (f32[4096]{0:T(1024)}, f32[128,50]{0,1:T(8,128)}, f32[50]{0:T(128)}) all-reduce(f32[4096]{0:T(1024)S(1)} %get-tuple-element.29, f32[128,50]{0,1:T(8,128)S(1)} %fusion.31, f32[50]{0:T(128)S(1)} %get-tuple-element.33), channel_id=1, replica_groups=mesh['dp_0'=4,'dp_1'=4,'hyper'=16] {'dp_0','dp_1','hyper'}, use_global_device_ids=true, to_apply=%region_5.6 | all-reduce | flops 10546 | bytes 84368 | tf_op jit(solution)/shard_map/psum | solution.py:98
  380.5 193.6 %all-reduce.4.cloned.1.call-done = (f32[128,4096]{0,1:T(8,128)}, f32[512,128]{1,0:T(8,128)}) async-done(((f32[128,4096]{0,1:T(8,128)}, f32[512,128]{1,0:T(8,128)}), (f32[128,4096]{0,1:T(8,128)}, f32[512,128]{1,0:T(8,128)})) %all-reduce.4.cloned.1.call-update) | async-done | bytes 2359312 | tf_op jit(solution)/shard_map/psum | solution.py:98
  574.1 2.9 copy.44
  577.0 43.1 %reduce-scatter.8.cloned.1.call-done = bf16[16,50,256]{2,1,0:T(8,128)(2,1)} async-done(((bf16[64,50,256]{2,1,0:T(8,128)(2,1)}), bf16[16,50,256]{2,1,0:T(8,128)(2,1)}) %reduce-scatter.8.cloned.1.call-update) | async-done | bytes 409616 | tf_op jit(solution)/shard_map/reduce_scatter | solution.py:31
  (48 shorter events, 18.3 us)
Async XLA Ops:
  7.2 13.3 %copy-start = (bf16[128,4096]{1,0:T(8,128)(2,1)S(1)}, bf16[128,4096]{1,0:T(8,128)(2,1)}, u32[]{:S(2)}) copy-start(bf16[128,4096]{1,0:T(8,128)(2,1)} %param.12) | copy-start | bytes 3145732
  8.5 22.3 %all-to-all-start.1 = ((s32[16,1,2]{2,1,0:T(1,128)}), s32[16,1,2]{2,1,0:T(1,128)S(1)}, u32[]{:S(2)}, u32[]{:S(2)}) async-start(s32[16,1,2]{2,1,0:T(1,128)} %broadcast_in_dim.2), calls=%async_computation.1 | async-start | bytes 16384 | tf_op jit(solution)/shard_map/all_to_all | solution.py:14
  28.6 13.2 %copy-start.8 = (bf16[512,128]{1,0:T(8,128)(2,1)S(1)}, bf16[512,128]{1,0:T(8,128)(2,1)}, u32[]{:S(2)}) copy-start(bf16[512,128]{1,0:T(8,128)(2,1)} %param.14) | copy-start | bytes 393220
  28.6 13.4 %copy-start.5 = (bf16[128,50]{0,1:T(8,128)(2,1)S(1)}, bf16[128,50]{0,1:T(8,128)(2,1)}, u32[]{:S(2)}) copy-start(bf16[128,50]{0,1:T(8,128)(2,1)} %param.15) | copy-start | bytes 38404
  28.6 13.4 %copy-start.7 = (f32[50]{0:T(128)S(1)}, f32[50]{0:T(128)}, u32[]{:S(2)}) copy-start(f32[50]{0:T(128)} %param.16) | copy-start | bytes 604
  30.9 32.3 %all-to-all-start = ((bf16[16,2,16384]{2,1,0:T(2,128)(2,1)}), bf16[16,2,16384]{2,1,0:T(2,128)(2,1)S(1)}, u32[]{:S(2)}, u32[]{:S(2)}) async-start(bf16[16,2,16384]{2,1,0:T(2,128)(2,1)} %reshape.50), calls=%async_computation | async-start | bytes 2097152 | tf_op jit(solution)/shard_map/all_to_all | solution.py:68
  40.5 127.2 %reduce-scatter.4.cloned.1.call-start = ((), (), s32[]{:S(2)}) async-start(), calls=%async_computation.6 | async-start | bytes 2228224 | tf_op jit(solution)/shard_map/reduce_scatter | solution.py:69
  76.0 91.6 %copy-start.9 = (s32[2,64]{1,0:T(2,128)S(1)}, s32[2,64]{1,0:T(2,128)}, u32[]{:S(2)}) copy-start(s32[2,64]{1,0:T(2,128)} %param.10) | copy-start | bytes 1540
  76.1 146.5 %all-gather.2.cloned.1.call-start = ((), (), s32[]{:S(2)}) async-start(), calls=%async_computation.7 | async-start | bytes 1114112 | tf_op jit(solution)/shard_map/all_gather | solution.py:76
  169.6 132.5 %reduce-scatter.6.cloned.1.call-start = ((), (), s32[]{:S(2)}) async-start(), calls=%async_computation.8 | async-start | bytes 9175040 | tf_op jit(solution)/shard_map/reduce_scatter | solution.py:31
  225.1 2.0 copy-start.1
  233.1 1.2 copy-start.2
  240.1 30.9 %all-to-all-start.2 = ((bf16[32,64,256]{2,1,0:T(8,128)(2,1)}), bf16[32,64,256]{2,1,0:T(8,128)(2,1)S(1)}, u32[]{:S(2)}, u32[]{:S(2)}) async-start(bf16[32,64,256]{2,1,0:T(8,128)(2,1)} %fusion.12), calls=%async_computation.3 | async-start | bytes 2097152 | tf_op jit(solution)/shard_map/all_to_all | solution.py:83
  243.9 330.2 %all-reduce.4.cloned.1.call-start = ((), (), s32[]{:S(2)}) async-start(), calls=%async_computation.10 | async-start | bytes 4718592 | tf_op jit(solution)/shard_map/psum | solution.py:98
  271.6 1.7 copy-start.3
  273.3 0.8 copy-start.6
  276.0 344.1 %reduce-scatter.8.cloned.1.call-start = ((), (), s32[]{:S(2)}) async-start(), calls=%async_computation.9 | async-start | bytes 2293760 | tf_op jit(solution)/shard_map/reduce_scatter | solution.py:31
  574.1 48.0 %copy-start.4 = (f32[512,128]{1,0:T(8,128)S(1)}, f32[512,128]{1,0:T(8,128)}, u32[]{:S(2)}) copy-start(f32[512,128]{1,0:T(8,128)} %get-tuple-element.39) | copy-start | bytes 786436
Sparse Core Ops, SparseCore 0:
  76.2 91.4 reduce-scatter.3
  170.9 51.5 all-gather.1
  233.3 68.8 reduce-scatter.5
  308.1 265.9 all-reduce.3
  576.5 43.5 reduce-scatter.7
where the time goes:
time: 631 us; the launch traced here: 629 us
  waiting for transfers between devices  418 us (66%)
  blocking collectives  78.2 us (12%)
  local copies, waits for them, and re-layouts  46.5 us (7%)
  matrix products  43.7 us (7%)
  starting transfers between devices  25.2 us (4%)
  between operations  14 us (2%)
    psum x1, waiting for transfers between devices, local(): lax.psum((grad_weight, grad_bias, grad_table, grad_in, grad_hbias), DP_HY...  194 us
    reduce_scatter x1, waiting for transfers between devices, local(): lax.psum_scatter(jnp.einsum('krd,kdc->krc', feat_cols, head_part, preferr...  91.6 us
    psum x1, blocking collectives, local(): lax.psum((grad_weight, grad_bias, grad_table, grad_in, grad_hbias), DP_HY...  78.2 us
    reduce_scatter x2, waiting for transfers between devices, own_rows(): total = lax.psum_scatter(total, axis, scatter_dimension=0, tiled=True)  69.2 us
    all_gather x1, waiting for transfers between devices, local(): dlog_rows = lax.all_gather(dlogits, 'hyper', axis=0, tiled=True)  52.8 us
    unnamed x27, local copies, waits for them, and re-layouts  26.5 us
  transfers between devices with their start and end apart: 8, of which 6 were waited for; matrix products, arithmetic and copies ran while one was open for 10% of the time, Pallas kernels for 0%

commit v1 on v0

v1 whole, which is shorter than its diff:
```python
import functools

import jax
import jax.numpy as jnp
from jax import lax
from jax.experimental import pallas as pl
from jax.experimental.pallas import tpu as pltpu
from jax.sharding import Mesh
from jax.sharding import PartitionSpec as P

AXES = ("x", "zl", "y", "zh", "core")
SIZES = (4, 4, 4, 2, 2)
HYPER = ("y", "zh", "core")
NDP = 16
PIECES = 4
MESH = pl.DeviceIdType.MESH
VMEM = pltpu.VMEM
F32 = jnp.float32
BF16 = jnp.bfloat16


def remote(src, dst, send, recv, device):
    return pltpu.make_async_remote_copy(
        src_ref=src, dst_ref=dst, send_sem=send, recv_sem=recv, device_id=device, device_id_type=MESH
    )


def hyper_place():
    y, zh, core = lax.axis_index("y"), lax.axis_index("zh"), lax.axis_index("core")
    y_peers = [{"y": lax.rem(y + o, 4)} for o in (1, 2, 3)]
    return y, zh, core, y_peers, {"zh": 1 - zh}, {"core": 1 - core}


def greet(devices):
    barrier = pltpu.get_barrier_semaphore()
    for device in devices:
        pl.semaphore_signal(barrier, inc=1, device_id=device, device_id_type=MESH)
    pl.semaphore_wait(barrier, len(devices))


class Gather:
    def __init__(self, buf, send, recv):
        self.buf, self.send, self.recv = buf, send, recv
        self.y, self.zh, self.core, self.y_peers, self.z_peer, self.c_peer = hyper_place()
        self.copies = {}

    def push(self, index, y, zh, device):
        block = self.buf.at[y, zh, self.core]
        copy = remote(block, block, self.send.at[index], self.recv.at[index], device)
        copy.start()
        self.copies[index] = copy

    def first(self):
        self.push(0, self.y, self.zh, self.z_peer)
        for i, peer in enumerate(self.y_peers):
            self.push(1 + i, self.y, self.zh, peer)
        self.push(7, self.y, self.zh, self.c_peer)

    def second(self):
        other = 1 - self.zh
        self.copies[0].wait_recv()
        for i, peer in enumerate(self.y_peers):
            self.push(4 + i, self.y, other, peer)
        self.push(8, self.y, other, self.c_peer)

    def third(self):
        for i in range(3):
            self.copies[1 + i].wait_recv()
            self.push(9 + i, lax.rem(self.y + 3 - i, 4), self.zh, self.c_peer)

    def fourth(self):
        for i in range(3):
            self.copies[4 + i].wait_recv()
            self.push(12 + i, lax.rem(self.y + 3 - i, 4), 1 - self.zh, self.c_peer)

    def last(self):
        for i in range(7, 15):
            self.copies[i].wait_recv()
        for i in range(15):
            self.copies[i].wait_send()


def gather_kernel(x_ref, ids_ref, x_out, ids_out, sx, rx, si, ri):
    y, zh, core, y_peers, z_peer, c_peer = hyper_place()
    ids_out[y, zh, core] = ids_ref[...]
    x_out[y, zh, core] = x_ref[...]
    greet([*y_peers, z_peer, c_peer])
    gathers = (Gather(ids_out, si, ri), Gather(x_out, sx, rx))
    for step in ("first", "second", "third", "fourth", "last"):
        for gather in gathers:
            getattr(gather, step)()


def logits_kernel(part, labels, out, r1, r2, r3, s2, c_send, c_recv, y_send, y_recv, z_send, z_recv, g_send, g_recv):
    y, zh, core, y_peers, z_peer, c_peer = hyper_place()
    greet([*y_peers, z_peer, c_peer])
    planes = (1 - zh, zh)
    copies = []
    for q, plane in enumerate(planes):
        copy = remote(part.at[:, plane, 1 - core], r1.at[plane], c_send.at[q], c_recv.at[q], c_peer)
        copy.start()
        copies.append(copy)
    y_copies = {}
    for q, plane in enumerate(planes):
        copies[q].wait_recv()
        for i, peer in enumerate(y_peers):
            to = lax.rem(y + 1 + i, 4)
            r1[plane, to] = r1[plane, to] + part[to, plane, core]
            copy = remote(r1.at[plane, to], r2.at[q, i], y_send.at[q, i], y_recv.at[q, i], peer)
            copy.start()
            y_copies[q, i] = copy
    total = r1[planes[0], y] + part[y, planes[0], core]
    for i in range(3):
        y_copies[0, i].wait_recv()
        total = total + r2[0, i]
    s2[...] = total
    z_copy = remote(s2, r3, z_send, z_recv, z_peer)
    z_copy.start()
    logits = r1[zh, y] + part[y, zh, core]
    for i in range(3):
        y_copies[1, i].wait_recv()
        logits = logits + r2[1, i]
    z_copy.wait_recv()
    logits = logits + r3[...]
    largest = jnp.max(logits, axis=-1, keepdims=True)
    exponent = jnp.exp(logits - largest)
    probability = exponent / jnp.sum(exponent, axis=-1, keepdims=True)
    classes = lax.broadcasted_iota(jnp.int32, logits.shape, 2)
    onehot = (labels[...] == classes).astype(F32)
    out[y, zh, core] = ((probability - onehot) / logits.shape[1]).astype(BF16)
    gather = Gather(out, g_send, g_recv)
    for step in ("first", "second", "third", "fourth", "last"):
        getattr(gather, step)()
    for copy in [*copies, *y_copies.values(), z_copy]:
        copy.wait_send()


def tail_kernel(
    g, e, gb, dhid, slope, ident, out, ew, gbh, hd,
    r1, rs, rd, tz, rz, re, gball, ha, hy, hz, hc,
    x1_s, x1_r, xs_s, xs_r, xd_s, xd_r, zz_s, zz_r,
    e_s, e_r, ea_s, ea_r, b_s, b_r, h_s, h_r, hx_s, hx_r, gw_s, gw_r, gg_s, gg_r,
):
    y, zh, core, y_peers, z_peer, c_peer = hyper_place()
    x, zl = lax.axis_index("x"), lax.axis_index("zl")
    dp = x * 4 + zl
    right, left = lax.rem(x + 1, 4), lax.rem(x + 3, 4)
    far = lax.rem(x + 2, 4)
    to_right, to_left = {"x": right}, {"x": left}

    def dp_device(o):
        to = lax.rem(dp + o, NDP)
        return to, {"x": to // 4, "zl": to % 4}

    greet([*y_peers, z_peer, c_peer, *[dp_device(o)[1] for o in range(1, NDP)]])

    c_copy = remote(dhid, hc, hx_s.at[0], hx_r.at[0], c_peer)
    c_copy.start()
    gball[dp] = gb[...]
    e_copies, b_copies = [], []
    for o in range(1, NDP):
        to, device = dp_device(o)
        copy = remote(e.at[to], re.at[o - 1], e_s.at[o - 1], e_r.at[o - 1], device)
        copy.start()
        e_copies.append(copy)
        copy = remote(gb, gball.at[dp], b_s.at[o - 1], b_r.at[o - 1], device)
        copy.start()
        b_copies.append(copy)

    rows = g.shape[2] // (2 * PIECES)
    cut = [pl.ds(p * rows, rows) for p in range(2 * PIECES)]
    far_copies, sum_copies, own_copies = {}, {}, {}
    order = [p for j in range(PIECES) for p in (j, PIECES + j)]
    for p in order:
        device = to_right if p < PIECES else to_left
        copy = remote(g.at[far, :, cut[p]], r1.at[p], x1_s.at[p], x1_r.at[p], device)
        copy.start()
        far_copies[p] = copy

    c_copy.wait_recv()
    ha[...] = dhid[...] + hc[...]
    hy_copies = []
    for i, peer in enumerate(y_peers):
        copy = remote(ha, hy.at[i], hx_s.at[1 + i], hx_r.at[1 + i], peer)
        copy.start()
        hy_copies.append(copy)
    partial = ha[...]
    for i in range(3):
        hy_copies[i].wait_recv()
        partial = partial + hy[i]
    hz[0] = partial
    hz_copy = remote(hz.at[0], hz.at[1], hx_s.at[4], hx_r.at[4], z_peer)
    hz_copy.start()

    total = e[dp]
    for o in range(1, NDP):
        e_copies[o - 1].wait_recv()
        total = total + re[o - 1]
    ew[y, zh, core, dp] = total.astype(BF16)
    ea_copies = []
    own_rows = ew.at[y, zh, core, dp]
    for o in range(1, NDP):
        copy = remote(own_rows, own_rows, ea_s.at[o - 1], ea_r.at[o - 1], dp_device(o)[1])
        copy.start()
        ea_copies.append(copy)
    bias = gb[...]
    for o in range(1, NDP):
        b_copies[o - 1].wait_recv()
    for i in range(1, NDP):
        bias = bias + gball[lax.rem(dp + i, NDP)]
    gbh[y, zh, core] = bias
    gb_gather = Gather(gbh, gg_s, gg_r)
    gb_gather.first()
    hz_copy.wait_recv()
    hd[dp] = (hz[0] + hz[1]) * slope[...] + ident[...]
    h_copies = []
    for o in range(1, NDP):
        copy = remote(hd.at[dp], hd.at[dp], h_s.at[o - 1], h_r.at[o - 1], dp_device(o)[1])
        copy.start()
        h_copies.append(copy)
    gb_gather.second()

    def passed_on(p):
        far_copies[p].wait_recv()
        if p < PIECES:
            chunk, device, back, other = right, to_right, left, to_left
        else:
            chunk, device, back, other = left, to_left, right, to_right
        r1[p] = (r1[p].astype(F32) + g[chunk, :, cut[p]].astype(F32)).astype(BF16)
        copy = remote(r1.at[p], rs.at[p], xs_s.at[p], xs_r.at[p], device)
        copy.start()
        sum_copies[p] = copy
        copy = remote(g.at[back, :, cut[p]], rd.at[p], xd_s.at[p], xd_r.at[p], other)
        copy.start()
        own_copies[p] = copy

    z_copies = {}

    def spread(p):
        sum_copies[p].wait_recv()
        own_copies[p].wait_recv()
        tz[p] = (g[x, :, cut[p]].astype(F32) + rs[p].astype(F32) + rd[p].astype(F32)).astype(BF16)
        for i in range(3):
            to = lax.rem(zl + 1 + i, 4)
            copy = remote(tz.at[p, to], rz.at[i, p], zz_s.at[i, p], zz_r.at[i, p], {"zl": to})
            copy.start()
            z_copies[i, p] = copy

    for p in order:
        passed_on(p)
    gw_gather = Gather(ew, gw_s, gw_r)
    gb_gather.third()
    gb_gather.fourth()
    for copy in ea_copies:
        copy.wait_recv()
    gw_gather.first()
    half = len(order) // 2
    for p in order[:half]:
        spread(p)
    gw_gather.second()
    for p in order[half:]:
        spread(p)
    gw_gather.third()
    gw_gather.fourth()
    for p in order:
        value = tz[p, zl].astype(F32)
        for i in range(3):
            z_copies[i, p].wait_recv()
            value = value + rz[i, p].astype(F32)
        out[cut[p]] = value

    for copy in h_copies:
        copy.wait_recv()
    gb_gather.last()
    gw_gather.last()
    sent = [c_copy, *e_copies, *b_copies, *far_copies.values(), *hy_copies, hz_copy, *ea_copies, *h_copies]
    for copy in [*sent, *sum_copies.values(), *own_copies.values(), *z_copies.values()]:
        copy.wait_send()


def call(kernel, outs, scratch, ident, args, limit, flops):
    size = sum(a.size * a.dtype.itemsize for a in [*args, *outs])
    return pl.pallas_call(
        kernel,
        out_shape=outs,
        in_specs=[pl.BlockSpec(memory_space=VMEM)] * len(args),
        out_specs=[pl.BlockSpec(memory_space=VMEM)] * len(outs),
        scratch_shapes=scratch,
        compiler_params=pltpu.CompilerParams(
            collective_id=ident, has_side_effects=True, vmem_limit_bytes=limit
        ),
        cost_estimate=pl.CostEstimate(flops=flops, bytes_accessed=size, transcendentals=0),
    )(*args)


def dma(*shape):
    return pltpu.SemaphoreType.DMA(shape)


def shape_of(shape, dtype):
    return jax.ShapeDtypeStruct(shape, dtype)


def gather_inputs(inputs, ids):
    outs = [shape_of((4, 2, 2, *inputs.shape), BF16), shape_of((4, 2, 2, *ids.shape), jnp.int32)]
    return call(gather_kernel, outs, [dma(15), dma(15), dma(15), dma(15)], 0, (inputs, ids), 16 << 20, 10**9)


def exchange_logits(part, labels):
    block = part.shape[3:]
    scratch = [
        VMEM((2, 4, *block), F32),
        VMEM((2, 3, *block), F32),
        VMEM(block, F32),
        VMEM(block, F32),
        dma(2), dma(2), dma(2, 3), dma(2, 3), pltpu.SemaphoreType.DMA, pltpu.SemaphoreType.DMA, dma(15), dma(15),
    ]
    outs = [shape_of((4, 2, 2, *block), BF16)]
    return call(logits_kernel, outs, scratch, 1, (part, labels), 32 << 20, 10**9)[0]


def tail(g, e, gb, dhid, slope, ident):
    rows, hh, cc = g.shape[2:]
    pieces = 2 * PIECES
    piece = (pieces, 4, rows // pieces, hh, cc)
    n = NDP - 1
    scratch = [
        VMEM(piece, BF16), VMEM(piece, BF16), VMEM(piece, BF16), VMEM(piece, BF16),
        VMEM((3, pieces, *piece[2:]), BF16),
        VMEM((n, *e.shape[1:]), F32),
        VMEM((NDP, *gb.shape), F32),
        VMEM(dhid.shape, F32), VMEM((3, *dhid.shape), F32), VMEM((2, *dhid.shape), F32), VMEM(dhid.shape, F32),
        dma(pieces), dma(pieces), dma(pieces), dma(pieces), dma(pieces), dma(pieces), dma(3, pieces), dma(3, pieces),
        dma(n), dma(n), dma(n), dma(n), dma(n), dma(n), dma(n), dma(n), dma(5), dma(5), dma(15), dma(15), dma(15), dma(15),
    ]
    outs = [
        shape_of((rows, hh, cc), F32),
        shape_of((4, 2, 2, *e.shape), BF16),
        shape_of((4, 2, 2, *gb.shape), F32),
        shape_of((NDP, *dhid.shape), F32),
    ]
    return call(tail_kernel, outs, scratch, 2, (g, e, gb, dhid, slope, ident), 48 << 20, 10**9)


def silu_slope(values):
    logistic = jax.nn.sigmoid(values)
    return logistic * (1.0 + values * (1.0 - logistic))


def pick(ids, embeddings):
    table_ids = jnp.arange(embeddings.shape[0], dtype=jnp.int32)
    select = (ids[:, None] == table_ids[None, :]).astype(BF16)
    return select, jnp.dot(select, embeddings, preferred_element_type=F32).astype(BF16)


def local(
    inputs, labels, client_ids, ext_weight, ext_bias, embeddings, hyper_in, hyper_bias, hyper_out
):
    own_slots, row_count, width_in = inputs.shape
    cols, hh, classes = hyper_out.shape
    slots = own_slots * 16
    hyper = lax.axis_index(HYPER)

    ids_tile = jnp.pad(client_ids[None, :], ((0, 7), (0, 128 - own_slots)))
    in_all, ids_all = gather_inputs(inputs, ids_tile)
    flat_in = in_all.reshape(slots * row_count, width_in)
    ids = ids_all[:, :, :, 0, :own_slots].reshape(slots)

    _, picked = pick(ids, embeddings)
    hyper_preact = jnp.dot(picked, hyper_in, preferred_element_type=F32) + hyper_bias
    hidden = jax.nn.silu(hyper_preact).astype(BF16)
    heads = jnp.einsum("kh,dhc->kdc", hidden, hyper_out, preferred_element_type=F32).astype(BF16)

    weight = lax.dynamic_slice_in_dim(ext_weight, hyper * cols, cols, 1)
    bias = lax.dynamic_slice_in_dim(ext_bias, hyper * cols, cols, 0)
    preact = jnp.dot(flat_in, weight, preferred_element_type=F32) + bias.astype(F32)
    features = jax.nn.silu(preact).astype(BF16).reshape(slots, row_count, cols)

    part = jnp.einsum("krd,kdc->krc", features, heads, preferred_element_type=F32)
    part = part.reshape(4, 2, 2, own_slots, row_count, classes)
    dlogits = exchange_logits(part, labels[:, :, None]).reshape(slots, row_count, classes)

    dheads = jnp.einsum("krd,krc->kdc", features, dlogits, preferred_element_type=F32).astype(BF16)
    dfeatures = jnp.einsum("krc,kdc->krd", dlogits, heads, preferred_element_type=F32).astype(BF16)
    dpreact = (dfeatures.reshape(slots * row_count, cols).astype(F32) * silu_slope(preact)).astype(BF16)
    grad_weight = jnp.dot(flat_in.T, dpreact, preferred_element_type=F32)
    grad_bias = jnp.sum(dpreact.astype(F32), axis=0)
    grad_out = jnp.einsum("kh,kdc->dhc", hidden, dheads, preferred_element_type=F32).astype(BF16)
    dhidden = jnp.einsum("kdc,dhc->kh", dheads, hyper_out, preferred_element_type=F32)

    lanes = ((0, 0), (0, 128 - hh))
    slope = jnp.pad(silu_slope(hyper_preact), lanes)
    ident = jnp.zeros((slots, 128), F32).at[:, 64].set(ids.astype(F32))
    grad_out, grad_weight, grad_bias, spread = tail(
        grad_out.reshape(4, 4, cols // NDP, hh, classes),
        grad_weight.reshape(NDP, width_in // NDP, cols),
        jnp.pad(grad_bias.reshape(cols // 128, 128), ((0, 8 - cols // 128), (0, 0))),
        jnp.pad(dhidden, lanes),
        slope,
        ident,
    )
    grad_weight = grad_weight.reshape(16, width_in, cols).transpose(1, 0, 2).reshape(width_in, 16 * cols).astype(F32)
    grad_bias = grad_bias[:, :, :, : cols // 128].reshape(16 * cols)

    spread = spread.reshape(NDP * slots, 128)
    every_id = spread[:, 64].astype(jnp.int32)
    hyper_dpre = spread[:, :hh]
    select, every_picked = pick(every_id, embeddings)
    highest = lax.Precision.HIGHEST
    grad_in = jnp.dot(every_picked.astype(F32).T, hyper_dpre, precision=highest)
    grad_hbias = jnp.sum(hyper_dpre, axis=0)
    back = jnp.dot(hyper_dpre, hyper_in.astype(F32).T, precision=highest)
    grad_table = jnp.dot(select.astype(F32).T, back, precision=highest)
    return grad_weight, grad_bias, grad_table, grad_in, grad_hbias, grad_out


def solution(mesh):
    torus = Mesh(mesh.devices.reshape(SIZES), AXES)
    placed = (P(AXES, None, None), P(AXES, None), P(AXES), P(), P(), P(), P(), P(), P(HYPER, None, None))
    return jax.shard_map(
        local,
        mesh=torus,
        in_specs=placed,
        out_specs=(P(), P(), P(), P(), P(), P((*HYPER, "x", "zl"), None, None)),
        check_vma=False,
    )
```

time: 631 us -> 208 us (0.33)
  waiting for transfers between devices: 418 us -> 0 us
  Pallas kernels: 0 us -> 136 us
  blocking collectives: 78.2 us -> 0 us
  starting transfers between devices: 25.2 us -> 0 us
  local copies, waits for them, and re-layouts: 46.5 us -> 29.3 us
  between operations: 14 us -> 0.79 us
  matrix products: 43.7 us -> 36.7 us
    psum x1 -> x0, waiting for transfers between devices: 194 us -> none  [local(): lax.psum((grad_weight, grad_bias, grad_table, grad_in, grad_hbias), DP_HY...]
    reduce_scatter x3 -> x0, waiting for transfers between devices: 161 us -> none  [the longest x1 91.6 us: local(): lax.psum_scatter(jnp.einsum('krd,kdc->krc', feat_cols, head_part, preferr...]
    pallas_call x0 -> x3, Pallas kernels: none -> 136 us  [call(): pl.pallas_call(kernel, out_shape=outs, in_specs=[pl.BlockSpec(memory_spac...]
    psum x1 -> x0, blocking collectives: 78.2 us -> none  [local(): lax.psum((grad_weight, grad_bias, grad_table, grad_in, grad_hbias), DP_HY...]
    all_gather x1 -> x0, waiting for transfers between devices: 52.8 us -> none  [local(): dlog_rows = lax.all_gather(dlogits, 'hyper', axis=0, tiled=True)]
    all_to_all x3 -> x0, starting transfers between devices: 24.6 us -> none  [the longest x1 11.2 us: sent_to_all(): return lax.all_to_all(copies, axis, split_axis=0, concat_axis=0, tiled=True)]
    all_to_all x3 -> x0, waiting for transfers between devices: 10.5 us -> none  [the longest x1 10.5 us: local(): lax.all_to_all(features, 'hyper', split_axis=2, concat_axis=0, tiled=True)]
    unnamed x27 -> x13, local copies, waits for them, and re-layouts: 26.5 us -> 16.4 us
  transfers between devices with their start and end apart: 8 -> 0, of which waited for: 6 -> 0; matrix products, arithmetic and copies ran while one was open for 10% -> 0% of each run, Pallas kernels for 0% -> 0%
where the time goes in v1:
time: 208 us; the launch traced here: 207 us
  Pallas kernels  136 us (65%)
  matrix products  36.7 us (18%)
  local copies, waits for them, and re-layouts  29.3 us (14%)
  other arithmetic  4.85 us (2%)
    pallas_call x3, Pallas kernels, call(): pl.pallas_call(kernel, out_shape=outs, in_specs=[pl.BlockSpec(memory_spac...  136 us
    unnamed x13, local copies, waits for them, and re-layouts  16.4 us
    dot_general x1, matrix products, local(): jnp.einsum('kh,kdc->dhc', hidden, dheads, preferred_element_type=F32)  8.21 us
    convert_element_type x1, local copies, waits for them, and re-layouts, local(): jnp.einsum('krd,krc->kdc', features, dlogits, preferred_element_type=F32)  7.96 us
    dot_general x1, matrix products, local(): jnp.einsum('kdc,dhc->kh', dheads, hyper_out, preferred_element_type=F32)  6.36 us
    dot_general x1, matrix products, local(): jnp.einsum('kh,dhc->kdc', hidden, hyper_out, preferred_element_type=F32)  5.57 us

profile of v1, /device:TPU:6, one launch (start us, length us, event | category | flops | bytes accessed | tf_op | source)
XLA Modules:
  0.0 207.1 jit_solution(4572457603793835234)
XLA Ops:
  2.7 0.8 copy.28.labels
  4.2 17.3 %shard_map.136 = (bf16[4,2,2,2,64,128]{5,4,3,2,1,0:T(8,128)(2,1)S(1)}, s32[4,2,2,8,128]{4,3,2,1,0:T(8,128)S(1)}) custom-call(bf16[2,64,128]{2,1,0:T(8,128)(2,1)S(1)} %copy-done.1, s32[8,128]{1,0:T(8,128)S(1)} %pad.18.ids_ref), custom_call_target="tpu_custom_call" | custom-call | flops 1000000000 | bytes 626688 | tf_op jit(solution)/shard_map/pallas_call | solution.py:283
  22.5 1.3 add_multiply_fusion
  23.8 1.0 copy.30
  25.5 2.1 %copy-done.2 = bf16[256,50,256]{2,0,1:T(8,128)(2,1)S(1)} copy-done((bf16[256,50,256]{2,0,1:T(8,128)(2,1)S(1)}, bf16[256,50,256]{2,0,1:T(8,128)(2,1)}, u32[]{:S(2)}) %copy-start.2) | copy-done | bytes 6553624
  27.6 5.6 %fusion.7 = bf16[32,256,256]{2,0,1:T(8,128)(2,1)S(1)} fusion(bf16[256,50,256]{2,0,1:T(8,128)(2,1)S(1)} %copy-done.2, f32[32,50]{1,0:T(8,128)S(1)} %get-tuple-element.47), kind=kOutput, calls=%fused_computation.9 | convolution fusion | flops 211820352 | bytes 10754304 | tf_op jit(solution)/shard_map/kh,dhc->kdc/dot_general | solution.py:372
  33.2 2.4 %fusion.5 = f32[32,64,256]{2,1,0:T(8,128)S(1)} fusion(bf16[32,64,256]{2,1,0:T(8,128)(2,1)S(1)} %bitcast.62, bf16[32,256,256]{2,0,1:T(8,128)(2,1)S(1)} %fusion.7), kind=kOutput, calls=%fused_computation.6 | convolution fusion | flops 268435456 | bytes 7340032 | tf_op jit(solution)/shard_map/krd,kdc->krc/dot_general | solution.py:379
  35.6 34.4 %shard_map.137 = bf16[4,2,2,2,64,256]{5,4,3,2,1,0:T(8,128)(2,1)S(1)} custom-call(f32[4,2,2,2,64,256]{5,4,3,2,1,0:T(8,128)S(1)} %bitcast.57, s32[2,64,1]{2,1,0:T(8,128)S(1)} %copy.28.labels), custom_call_target="tpu_custom_call" | custom-call | flops 1000000000 | bytes 3146240 | tf_op jit(solution)/shard_map/pallas_call | solution.py:283
  70.1 2.5 %fusion.11 = bf16[32,64,256]{2,1,0:T(8,128)(2,1)S(1)} fusion(bf16[32,64,256]{2,1,0:T(8,128)(2,1)S(1)} %bitcast.55, bf16[32,256,256]{2,0,1:T(8,128)(2,1)S(1)} %fusion.7), kind=kOutput, calls=%fused_computation.17 | convolution fusion | flops 268959744 | bytes 6291456 | tf_op jit(solution)/shard_map/krc,kdc->krd/dot_general | solution.py:384
  72.6 1.1 convert_reduce_fusion
  74.1 3.4 %convolution_convert_fusion.1 = bf16[32,256,256]{2,1,0:T(8,128)(2,1)} fusion(bf16[32,64,256]{2,1,0:T(8,128)(2,1)S(1)} %bitcast.63, bf16[32,64,256]{2,1,0:T(8,128)(2,1)S(1)} %bitcast.56), kind=kOutput, calls=%fused_computation.10 | convolution fusion | flops 270532608 | bytes 6291456 | tf_op jit(solution)/shard_map/krd,krc->kdc/dot_general | solution.py:383
  77.5 8.0 %copy.32 = bf16[32,256,256]{1,0,2:T(8,128)(2,1)} copy(bf16[32,256,256]{2,1,0:T(8,128)(2,1)} %convolution_convert_fusion.1) | data formatting | bytes 8388608 | tf_op jit(solution)/shard_map/convert_element_type | solution.py:383
  85.4 8.2 %convolution_convert_fusion = bf16[256,256,50]{1,2,0:T(8,128)(2,1)} fusion(bf16[32,256,256]{2,1,0:T(8,128)(2,1)} %convolution_convert_fusion.1, f32[32,50]{1,0:T(8,128)S(1)} %get-tuple-element.47), kind=kOutput, calls=%fused_computation.2 | convolution fusion | flops 213000000 | bytes 10754304 | tf_op jit(solution)/shard_map/kh,kdc->dhc/dot_general | solution.py:388
  93.6 11.3 %copy.33 = bf16[256,50,256]{0,1,2:T(8,128)(2,1)} copy(bf16[256,50,256]{2,0,1:T(8,128)(2,1)} %param.19) | data formatting | bytes 13107200 | tf_op args[8]
  105.0 6.4 %convolution_bitcast_fusion = f32[32,50]{1,0:T(8,128)S(1)} fusion(bf16[32,256,256]{1,0,2:T(8,128)(2,1)} %copy.32, bf16[256,50,256]{0,1,2:T(8,128)(2,1)} %copy.33), kind=kOutput, calls=%fused_computation.19 | convolution fusion | flops 209715200 | bytes 10754304 | tf_op jit(solution)/shard_map/kdc,dhc->kh/dot_general | solution.py:389
  111.4 83.8 %shard_map.138 = (f32[16,50,256]{2,1,0:T(8,128)S(1)}, bf16[4,2,2,16,8,256]{5,4,3,2,1,0:T(8,128)(2,1)S(1)}, f32[4,2,2,8,128]{4,3,2,1,0:T(8,128)S(1)}, f32[16,32,128]{2,1,0:T(8,128)S(1)}) custom-call(bf16[4,4,16,50,256]{4,3,2,1,0:T(8,128)(2,1)} %bitcast.61, f32[16,8,256]{2,1,0:T(8,128)S(1)} %fusion.14.e, f32[8,128]{1,0:T(8,128)S(1)} %pad.19.gb, ...), custom_call_target="tpu_custom_call" | custom-call | flops 1000000000 | bytes 8933376 | tf_op jit(solution)/shard_map/pallas_call | solution.py:283
  196.4 1.0 fusion.22
  197.4 0.8 slice_convert_fusion
  198.2 1.1 copy.40
  199.3 2.8 %fusion.16 = f32[512,128]{1,0:T(8,128)} fusion(f32[512,128]{1,0:T(8,128)} %fusion.22, s32[512]{0:T(512)S(1)} %bitcast.66), kind=kOutput, calls=%fused_computation.25 | convolution fusion | flops 402915328 | bytes 526336 | tf_op jit(solution)/shard_map/dot_general | solution.py:413
  202.0 1.3 convolution_convert_fusion.2
  203.3 1.0 fusion.20
  204.3 1.1 copy.37
  205.6 1.5 copy.39
  (25 shorter events, 6.2 us)
Async XLA Ops:
  0.6 24.2 %copy-start = (bf16[128,4096]{1,0:T(8,128)(2,1)S(1)}, bf16[128,4096]{1,0:T(8,128)(2,1)}, u32[]{:S(2)}) copy-start(bf16[128,4096]{1,0:T(8,128)(2,1)} %param.14) | copy-start | bytes 3145732
  3.5 0.8 copy-start.1
  24.8 2.9 %copy-start.2 = (bf16[256,50,256]{2,0,1:T(8,128)(2,1)S(1)}, bf16[256,50,256]{2,0,1:T(8,128)(2,1)}, u32[]{:S(2)}) copy-start(bf16[256,50,256]{2,0,1:T(8,128)(2,1)} %param.19) | copy-start | bytes 19660804
  70.1 3.7 %copy-start.3 = (bf16[128,2048]{1,0:T(8,128)(2,1)S(1)}, bf16[128,2048]{1,0:T(8,128)(2,1)}, u32[]{:S(2)}) copy-start(bf16[128,2048]{1,0:T(8,128)(2,1)} %copy.30) | copy-start | bytes 1572868
  111.3 85.1 %copy-start.4 = (bf16[128,50]{0,1:T(8,128)(2,1)S(1)}, bf16[128,50]{0,1:T(8,128)(2,1)}, u32[]{:S(2)}) copy-start(bf16[128,50]{0,1:T(8,128)(2,1)} %param.17) | copy-start | bytes 38404

commit v2 on v1

--- a/solution.py
+++ b/solution.py
@@ -12,7 +12,8 @@
 SIZES = (4, 4, 4, 2, 2)
 HYPER = ("y", "zh", "core")
 NDP = 16
-PIECES = 4
+HH = 50
+HP = 64
 MESH = pl.DeviceIdType.MESH
 VMEM = pltpu.VMEM
 F32 = jnp.float32
@@ -135,18 +136,33 @@
         copy.wait_send()
 
 
+def iota(shape, dim):
+    return lax.broadcasted_iota(jnp.int32, shape, dim)
+
+
+def onehot(mask, dtype=BF16):
+    return jnp.where(mask, jnp.ones(mask.shape, F32), jnp.zeros(mask.shape, F32)).astype(dtype)
+
+
+def dot(a, b, dims, precision=None):
+    return lax.dot_general(a, b, ((dims[:1], dims[1:]), ((), ())), precision=precision, preferred_element_type=F32)
+
+
 def tail_kernel(
-    g, e, gb, dhid, slope, ident, out, ew, gbh, hd,
-    r1, rs, rd, tz, rz, re, gball, ha, hy, hz, hc,
+    feat, dl, heads, slope, flat_in, w, hid, hslope, ident, emb, hin,
+    out, gw_out, gb_out, table_out, gin_out, ghb_out,
+    dh, block, acc, g, r1, rs, rd, tz, rz, e, re, gb, gball, ew, gbh, hd, dhid, ha, hy, hz, hc,
     x1_s, x1_r, xs_s, xs_r, xd_s, xd_r, zz_s, zz_r,
     e_s, e_r, ea_s, ea_r, b_s, b_r, h_s, h_r, hx_s, hx_r, gw_s, gw_r, gg_s, gg_r,
 ):
     y, zh, core, y_peers, z_peer, c_peer = hyper_place()
     x, zl = lax.axis_index("x"), lax.axis_index("zl")
     dp = x * 4 + zl
-    right, left = lax.rem(x + 1, 4), lax.rem(x + 3, 4)
-    far = lax.rem(x + 2, 4)
-    to_right, to_left = {"x": right}, {"x": left}
+    right, left, far = lax.rem(x + 1, 4), lax.rem(x + 3, 4), lax.rem(x + 2, 4)
+    toward = ({"x": right}, {"x": left})
+    slots, row_count, cols = feat.shape
+    classes = dl.shape[2]
+    hh, hp = HH, HP
 
     def dp_device(o):
         to = lax.rem(dp + o, NDP)
@@ -154,8 +170,96 @@
 
     greet([*y_peers, z_peer, c_peer, *[dp_device(o)[1] for o in range(1, NDP)]])
 
-    c_copy = remote(dhid, hc, hx_s.at[0], hx_r.at[0], c_peer)
-    c_copy.start()
+    row, col = iota((8 * hh, hp), 0), iota((8 * hh, hp), 1)
+    group = sum((row >= hh * j).astype(jnp.int32) for j in range(1, 8))
+    spread_h = onehot(row - hh * group == col)
+    by_slot = dot(spread_h, hid[...], (1, 1)).astype(BF16)
+    row, col = iota((slots, 8 * slots), 0), iota((slots, 8 * slots), 1)
+    spread_k = onehot(row == (col >> 3))
+    full = dot(by_slot, spread_k, (1, 0))
+    row, col = iota(full.shape, 0), iota(full.shape, 1)
+    group = sum((row >= hh * j).astype(jnp.int32) for j in range(1, 8))
+    block[...] = jnp.where(group == (col & 7), full, jnp.zeros_like(full)).astype(BF16)
+
+    def one_slot(k, carry):
+        dh[k] = dot(feat[k], dl[k], (0, 0)).astype(BF16).astype(F32)
+        return carry
+
+    lax.fori_loop(0, slots, one_slot, 0)
+
+    def rows_of(d0):
+        return dh[:, pl.ds(pl.multiple_of(d0, 8), 8), :].reshape(8 * slots, classes).astype(BF16)
+
+    z_target = [lax.rem(zl + o, 4) for o in (2, 1, 3, 0)]
+
+    def z_of(q):
+        if isinstance(q, int):
+            return z_target[q]
+        return jnp.where(q == 0, z_target[0], jnp.where(q == 1, z_target[1], jnp.where(q == 2, z_target[2], z_target[3])))
+
+    def piece(chunk, q, half):
+        zt = z_of(q)
+        x8 = rows_of((chunk * 4 + zt) * 16 + half * 8)
+        g[chunk, zt, half] = jnp.dot(block[...], x8, preferred_element_type=F32).astype(BF16)
+
+    def far_copy(half, q):
+        return remote(g.at[far, z_of(q), half], r1.at[half, q], x1_s.at[half, q], x1_r.at[half, q], toward[half])
+
+    def own_copy(half, q):
+        chunk = left if half == 0 else right
+        return remote(g.at[chunk, z_of(q), half], rd.at[half, q], xd_s.at[half, q], xd_r.at[half, q], toward[1 - half])
+
+    def sum_copy(half, q):
+        return remote(r1.at[half, q], rs.at[half, q], xs_s.at[half, q], xs_r.at[half, q], toward[half])
+
+    def z_copy(half, q):
+        return remote(tz.at[half, q], rz.at[half, q], zz_s.at[half, q], zz_r.at[half, q], {"zl": z_of(q)})
+
+    def both(make, q):
+        for half in range(2):
+            make(half, q).start()
+
+    def passed_on(q):
+        for half in range(2):
+            far_copy(half, q).wait_recv()
+            chunk = right if half == 0 else left
+            r1[half, q] = (r1[half, q].astype(F32) + g[chunk, z_of(q), half].astype(F32)).astype(BF16)
+            sum_copy(half, q).start()
+
+    def spread(q):
+        for half in range(2):
+            sum_copy(half, q).wait_recv()
+            own_copy(half, q).wait_recv()
+            total = g[x, z_of(q), half].astype(F32) + rs[half, q].astype(F32) + rd[half, q].astype(F32)
+            tz[half, q] = total.astype(BF16)
+            if q < 3:
+                z_copy(half, q).start()
+
+    def pieces(chunks, q):
+        for chunk in chunks:
+            for half in range(2):
+                piece(chunk, q, half)
+
+    for q in range(2):
+        pieces((far,), q)
+        both(far_copy, q)
+
+    e[...] = jnp.zeros_like(e)
+    gb[...] = jnp.zeros_like(gb)
+
+    def four_slots(i, carry):
+        parts = []
+        for j in range(4):
+            k = i * 4 + j
+            dfeat = dot(dl[k], heads[k], (1, 1)).astype(BF16).astype(F32)
+            parts.append((dfeat * slope[k]).astype(BF16))
+        dpre = jnp.concatenate(parts, axis=0)
+        here = flat_in[pl.ds(pl.multiple_of(i * 4 * row_count, 4 * row_count), 4 * row_count), :]
+        e[...] += dot(here, dpre, (0, 0)).reshape(e.shape)
+        gb[...] += jnp.sum(dpre.astype(F32), axis=0, keepdims=True)
+        return carry
+
+    lax.fori_loop(0, slots // 4, four_slots, 0)
     gball[dp] = gb[...]
     e_copies, b_copies = [], []
     for o in range(1, NDP):
@@ -167,15 +271,49 @@
         copy.start()
         b_copies.append(copy)
 
-    rows = g.shape[2] // (2 * PIECES)
-    cut = [pl.ds(p * rows, rows) for p in range(2 * PIECES)]
-    far_copies, sum_copies, own_copies = {}, {}, {}
-    order = [p for j in range(PIECES) for p in (j, PIECES + j)]
-    for p in order:
-        device = to_right if p < PIECES else to_left
-        copy = remote(g.at[far, :, cut[p]], r1.at[p], x1_s.at[p], x1_r.at[p], device)
-        copy.start()
-        far_copies[p] = copy
+    def rest(q, carry):
+        pieces((right, left), q)
+        return carry
+
+    lax.fori_loop(0, 4, rest, 0)
+    both(own_copy, 0)
+    for q in (2, 3):
+        pieces((far,), q)
+    passed_on(0)
+    both(far_copy, 2)
+    both(own_copy, 1)
+
+    def own_pieces(q, carry):
+        pieces((x,), q)
+        return carry
+
+    lax.fori_loop(0, 4, own_pieces, 0)
+
+    acc[...] = jnp.zeros_like(acc)
+    gap = jnp.zeros((8, hp - hh, classes), BF16)
+
+    def two_groups(i, carry):
+        value = acc[...]
+        for j in range(2):
+            d0 = (i * 2 + j) * 8
+            w8 = jnp.concatenate([w[pl.ds(d0, 8)], gap], axis=1).reshape(8 * hp, classes)
+            value = value + dot(rows_of(d0), w8, (1, 1))
+        acc[...] = value
+        return carry
+
+    lax.fori_loop(0, cols // 16, two_groups, 0)
+    highest = lax.Precision.HIGHEST
+    row, col = iota(acc.shape, 0), iota(acc.shape, 1)
+    kept = jnp.where((row & 7) == (col >> 6), acc[...], jnp.zeros_like(acc[...]))
+    by_k = dot(onehot(iota((slots, 8 * slots), 0) == (iota((slots, 8 * slots), 1) >> 3), F32), kept, (1, 0), highest)
+    fold = onehot((iota((8 * hp, 128), 0) & (hp - 1)) == iota((8 * hp, 128), 1), F32)
+    dhid[...] = dot(by_k, fold, (1, 0), highest)
+    c_copy = remote(dhid, hc, hx_s.at[0], hx_r.at[0], c_peer)
+    c_copy.start()
+
+    passed_on(1)
+    both(far_copy, 3)
+    both(own_copy, 2)
 
     c_copy.wait_recv()
     ha[...] = dhid[...] + hc[...]
@@ -184,6 +322,26 @@
         copy = remote(ha, hy.at[i], hx_s.at[1 + i], hx_r.at[1 + i], peer)
         copy.start()
         hy_copies.append(copy)
+
+    total = e[dp]
+    for o in range(1, NDP):
+        e_copies[o - 1].wait_recv()
+        total = total + re[o - 1]
+    ew[y, zh, core, dp] = total.astype(BF16)
+    own_rows = ew.at[y, zh, core, dp]
+    ea_copies = []
+    for o in range(1, NDP):
+        copy = remote(own_rows, own_rows, ea_s.at[o - 1], ea_r.at[o - 1], dp_device(o)[1])
+        copy.start()
+        ea_copies.append(copy)
+    bias = gb[...]
+    for o in range(1, NDP):
+        b_copies[o - 1].wait_recv()
+        bias = bias + gball[lax.rem(dp + NDP - o, NDP)]
+    gbh[y, zh, core] = bias
+    gb_gather = Gather(gbh, gg_s, gg_r)
+    gb_gather.first()
+
     partial = ha[...]
     for i in range(3):
         hy_copies[i].wait_recv()
@@ -191,90 +349,71 @@
     hz[0] = partial
     hz_copy = remote(hz.at[0], hz.at[1], hx_s.at[4], hx_r.at[4], z_peer)
     hz_copy.start()
-
-    total = e[dp]
-    for o in range(1, NDP):
-        e_copies[o - 1].wait_recv()
-        total = total + re[o - 1]
-    ew[y, zh, core, dp] = total.astype(BF16)
-    ea_copies = []
-    own_rows = ew.at[y, zh, core, dp]
-    for o in range(1, NDP):
-        copy = remote(own_rows, own_rows, ea_s.at[o - 1], ea_r.at[o - 1], dp_device(o)[1])
-        copy.start()
-        ea_copies.append(copy)
-    bias = gb[...]
-    for o in range(1, NDP):
-        b_copies[o - 1].wait_recv()
-    for i in range(1, NDP):
-        bias = bias + gball[lax.rem(dp + i, NDP)]
-    gbh[y, zh, core] = bias
-    gb_gather = Gather(gbh, gg_s, gg_r)
-    gb_gather.first()
+    gb_gather.second()
+
+    spread(0)
+    passed_on(2)
+    both(own_copy, 3)
+
     hz_copy.wait_recv()
-    hd[dp] = (hz[0] + hz[1]) * slope[...] + ident[...]
+    hd[dp] = (hz[0] + hz[1]) * hslope[...] + ident[...]
     h_copies = []
     for o in range(1, NDP):
         copy = remote(hd.at[dp], hd.at[dp], h_s.at[o - 1], h_r.at[o - 1], dp_device(o)[1])
         copy.start()
         h_copies.append(copy)
-    gb_gather.second()
-
-    def passed_on(p):
-        far_copies[p].wait_recv()
-        if p < PIECES:
-            chunk, device, back, other = right, to_right, left, to_left
-        else:
-            chunk, device, back, other = left, to_left, right, to_right
-        r1[p] = (r1[p].astype(F32) + g[chunk, :, cut[p]].astype(F32)).astype(BF16)
-        copy = remote(r1.at[p], rs.at[p], xs_s.at[p], xs_r.at[p], device)
-        copy.start()
-        sum_copies[p] = copy
-        copy = remote(g.at[back, :, cut[p]], rd.at[p], xd_s.at[p], xd_r.at[p], other)
-        copy.start()
-        own_copies[p] = copy
-
-    z_copies = {}
-
-    def spread(p):
-        sum_copies[p].wait_recv()
-        own_copies[p].wait_recv()
-        tz[p] = (g[x, :, cut[p]].astype(F32) + rs[p].astype(F32) + rd[p].astype(F32)).astype(BF16)
-        for i in range(3):
-            to = lax.rem(zl + 1 + i, 4)
-            copy = remote(tz.at[p, to], rz.at[i, p], zz_s.at[i, p], zz_r.at[i, p], {"zl": to})
-            copy.start()
-            z_copies[i, p] = copy
-
-    for p in order:
-        passed_on(p)
-    gw_gather = Gather(ew, gw_s, gw_r)
     gb_gather.third()
     gb_gather.fourth()
     for copy in ea_copies:
         copy.wait_recv()
+    gw_gather = Gather(ew, gw_s, gw_r)
     gw_gather.first()
-    half = len(order) // 2
-    for p in order[:half]:
-        spread(p)
+
+    spread(1)
+    passed_on(3)
     gw_gather.second()
-    for p in order[half:]:
-        spread(p)
     gw_gather.third()
-    gw_gather.fourth()
-    for p in order:
-        value = tz[p, zl].astype(F32)
-        for i in range(3):
-            z_copies[i, p].wait_recv()
-            value = value + rz[i, p].astype(F32)
-        out[cut[p]] = value
 
     for copy in h_copies:
         copy.wait_recv()
+    every = hd[...].reshape(NDP * slots, 128)
+    lane = iota(every.shape, 1)
+    hyper_dpre = jnp.where(lane < hh, every, jnp.zeros_like(every))
+    clients = emb.shape[0]
+    same = iota((NDP * slots, clients), 1).astype(F32) == every[:, 64:65]
+    select = onehot(same, F32)
+    picked = dot(select.astype(BF16), emb[...], (1, 0))
+    gin_out[...] = dot(picked, hyper_dpre, (0, 0), highest)
+    ghb_out[...] = jnp.sum(hyper_dpre, axis=0, keepdims=True)
+    back = dot(hyper_dpre, hin[...].astype(F32), (1, 1), highest)
+    table_out[...] = dot(select, back, (0, 0), highest)
+
+    spread(2)
+    gw_gather.fourth()
+    spread(3)
     gb_gather.last()
+    for i in range(16):
+        at = (i // 4, (i // 2) % 2, i % 2)
+        gb_out[:, i * cols : (i + 1) * cols] = gbh[at]
     gw_gather.last()
-    sent = [c_copy, *e_copies, *b_copies, *far_copies.values(), *hy_copies, hz_copy, *ea_copies, *h_copies]
-    for copy in [*sent, *sum_copies.values(), *own_copies.values(), *z_copies.values()]:
+    for i in range(16):
+        at = (i // 4, (i // 2) % 2, i % 2)
+        gw_out[:, i * cols : (i + 1) * cols] = ew[at].astype(F32).reshape(-1, cols)
+    for half in range(2):
+        value = tz[half, 3].astype(F32)
+        for q in range(3):
+            z_copy(half, q).wait_recv()
+            value = value + rz[half, q].astype(F32)
+        for j in range(8):
+            out[half * 8 + j] = value[j * hh : (j + 1) * hh]
+
+    for half in range(2):
+        for q in range(4):
+            for make in (far_copy, own_copy, sum_copy):
+                make(half, q).wait_send()
+            if q < 3:
+                z_copy(half, q).wait_send()
+    for copy in [c_copy, *e_copies, *b_copies, *hy_copies, hz_copy, *ea_copies, *h_copies]:
         copy.wait_send()
 
 
@@ -319,27 +458,39 @@
     return call(logits_kernel, outs, scratch, 1, (part, labels), 32 << 20, 10**9)[0]
 
 
-def tail(g, e, gb, dhid, slope, ident):
-    rows, hh, cc = g.shape[2:]
-    pieces = 2 * PIECES
-    piece = (pieces, 4, rows // pieces, hh, cc)
+def tail(feat, dl, heads, slope, flat_in, w, hid, hslope, ident, emb, hin):
+    slots, row_count, cols = feat.shape
+    classes = dl.shape[2]
+    width_in = flat_in.shape[1]
+    piece = (8 * HH, classes)
     n = NDP - 1
+    rows = (NDP, width_in // NDP, cols)
+    lanes = hslope.shape
     scratch = [
-        VMEM(piece, BF16), VMEM(piece, BF16), VMEM(piece, BF16), VMEM(piece, BF16),
-        VMEM((3, pieces, *piece[2:]), BF16),
-        VMEM((n, *e.shape[1:]), F32),
-        VMEM((NDP, *gb.shape), F32),
-        VMEM(dhid.shape, F32), VMEM((3, *dhid.shape), F32), VMEM((2, *dhid.shape), F32), VMEM(dhid.shape, F32),
-        dma(pieces), dma(pieces), dma(pieces), dma(pieces), dma(pieces), dma(pieces), dma(3, pieces), dma(3, pieces),
+        VMEM((slots, cols, classes), F32),
+        VMEM((8 * HH, 8 * slots), BF16),
+        VMEM((8 * slots, 8 * HP), F32),
+        VMEM((4, 4, 2, *piece), BF16),
+        VMEM((2, 4, *piece), BF16), VMEM((2, 4, *piece), BF16), VMEM((2, 4, *piece), BF16), VMEM((2, 4, *piece), BF16),
+        VMEM((2, 3, *piece), BF16),
+        VMEM(rows, F32), VMEM((n, *rows[1:]), F32),
+        VMEM((1, cols), F32), VMEM((NDP, 1, cols), F32),
+        VMEM((4, 2, 2, *rows), BF16), VMEM((4, 2, 2, 1, cols), F32),
+        VMEM((NDP, *lanes), F32),
+        VMEM(lanes, F32), VMEM(lanes, F32), VMEM((3, *lanes), F32), VMEM((2, *lanes), F32), VMEM(lanes, F32),
+        dma(2, 4), dma(2, 4), dma(2, 4), dma(2, 4), dma(2, 4), dma(2, 4), dma(2, 3), dma(2, 3),
         dma(n), dma(n), dma(n), dma(n), dma(n), dma(n), dma(n), dma(n), dma(5), dma(5), dma(15), dma(15), dma(15), dma(15),
     ]
     outs = [
-        shape_of((rows, hh, cc), F32),
-        shape_of((4, 2, 2, *e.shape), BF16),
-        shape_of((4, 2, 2, *gb.shape), F32),
-        shape_of((NDP, *dhid.shape), F32),
+        shape_of((16, HH, classes), F32),
+        shape_of((width_in, 16 * cols), F32),
+        shape_of((1, 16 * cols), F32),
+        shape_of(emb.shape, F32),
+        shape_of((emb.shape[1], 128), F32),
+        shape_of((1, 128), F32),
     ]
-    return call(tail_kernel, outs, scratch, 2, (g, e, gb, dhid, slope, ident), 48 << 20, 10**9)
+    args = (feat, dl, heads, slope, flat_in, w, hid, hslope, ident, emb, hin)
+    return call(tail_kernel, outs, scratch, 2, args, 64000 << 10, 10**10)
 
 
 def silu_slope(values):
@@ -380,38 +531,23 @@
     part = part.reshape(4, 2, 2, own_slots, row_count, classes)
     dlogits = exchange_logits(part, labels[:, :, None]).reshape(slots, row_count, classes)
 
-    dheads = jnp.einsum("krd,krc->kdc", features, dlogits, preferred_element_type=F32).astype(BF16)
-    dfeatures = jnp.einsum("krc,kdc->krd", dlogits, heads, preferred_element_type=F32).astype(BF16)
-    dpreact = (dfeatures.reshape(slots * row_count, cols).astype(F32) * silu_slope(preact)).astype(BF16)
-    grad_weight = jnp.dot(flat_in.T, dpreact, preferred_element_type=F32)
-    grad_bias = jnp.sum(dpreact.astype(F32), axis=0)
-    grad_out = jnp.einsum("kh,kdc->dhc", hidden, dheads, preferred_element_type=F32).astype(BF16)
-    dhidden = jnp.einsum("kdc,dhc->kh", dheads, hyper_out, preferred_element_type=F32)
-
     lanes = ((0, 0), (0, 128 - hh))
-    slope = jnp.pad(silu_slope(hyper_preact), lanes)
+    hslope = jnp.pad(silu_slope(hyper_preact), lanes)
     ident = jnp.zeros((slots, 128), F32).at[:, 64].set(ids.astype(F32))
-    grad_out, grad_weight, grad_bias, spread = tail(
-        grad_out.reshape(4, 4, cols // NDP, hh, classes),
-        grad_weight.reshape(NDP, width_in // NDP, cols),
-        jnp.pad(grad_bias.reshape(cols // 128, 128), ((0, 8 - cols // 128), (0, 0))),
-        jnp.pad(dhidden, lanes),
-        slope,
+    grad_out, grad_weight, grad_bias, grad_table, grad_in, grad_hbias = tail(
+        features,
+        dlogits,
+        heads,
+        silu_slope(preact).reshape(features.shape),
+        flat_in,
+        hyper_out,
+        jnp.pad(hidden, ((0, 0), (0, HP - hh))),
+        hslope,
         ident,
+        embeddings,
+        jnp.pad(hyper_in, lanes),
     )
-    grad_weight = grad_weight.reshape(16, width_in, cols).transpose(1, 0, 2).reshape(width_in, 16 * cols).astype(F32)
-    grad_bias = grad_bias[:, :, :, : cols // 128].reshape(16 * cols)
-
-    spread = spread.reshape(NDP * slots, 128)
-    every_id = spread[:, 64].astype(jnp.int32)
-    hyper_dpre = spread[:, :hh]
-    select, every_picked = pick(every_id, embeddings)
-    highest = lax.Precision.HIGHEST
-    grad_in = jnp.dot(every_picked.astype(F32).T, hyper_dpre, precision=highest)
-    grad_hbias = jnp.sum(hyper_dpre, axis=0)
-    back = jnp.dot(hyper_dpre, hyper_in.astype(F32).T, precision=highest)
-    grad_table = jnp.dot(select.astype(F32).T, back, precision=highest)
-    return grad_weight, grad_bias, grad_table, grad_in, grad_hbias, grad_out
+    return grad_weight, grad_bias[0], grad_table, grad_in[:, :hh], grad_hbias[0, :hh], grad_out
 
 
 def solution(mesh):

time: 208 us -> 189 us (0.909); the launches traced: 207 us -> 186 us
  matrix products: 36.7 us -> 10.7 us
  Pallas kernels: 136 us -> 144 us
  other arithmetic: 4.85 us -> 2.1 us
    dot_general x9 -> x0, matrix products: 26.7 us -> none  [the longest x1 8.21 us: local(): jnp.einsum('kh,kdc->dhc', hidden, dheads, preferred_element_type=F32)]
    convert_element_type x2 -> x0, local copies, waits for them, and re-layouts: 9.49 us -> none  [the longest x1 7.96 us: local(): jnp.einsum('krd,krc->kdc', features, dlogits, preferred_element_type=F32)]
    pallas_call x3, Pallas kernels: 136 us -> 144 us  [call(): pl.pallas_call(kernel, out_shape=outs, in_specs=[pl.BlockSpec(memory_spac...]
    dot_general x1, local copies, waits for them, and re-layouts: 1.01 us -> 4.51 us  [local(): jnp.einsum('kh,dhc->kdc', hidden, hyper_out, preferred_element_type=F32)]
    unnamed x13 -> x31, local copies, waits for them, and re-layouts: 16.4 us -> 18.6 us
where the time goes in v2:
time: 189 us; the launch traced here: 186 us
  Pallas kernels  144 us (76%)
  local copies, waits for them, and re-layouts  28.4 us (15%)
  matrix products  10.7 us (6%)
  other arithmetic  2.1 us (1%)
    pallas_call x3, Pallas kernels, call(): pl.pallas_call(kernel, out_shape=outs, in_specs=[pl.BlockSpec(memory_spac...  144 us
    unnamed x31, local copies, waits for them, and re-layouts  18.6 us
    dot_general x1, matrix products, local(): jnp.einsum('kh,dhc->kdc', hidden, hyper_out, preferred_element_type=F32)  5.55 us
    dot_general x1, local copies, waits for them, and re-layouts, local(): jnp.einsum('kh,dhc->kdc', hidden, hyper_out, preferred_element_type=F32)  4.51 us

profile of v2, /device:TPU:6, one launch (start us, length us, event | category | flops | bytes accessed | tf_op | source)
XLA Modules:
  0.0 185.7 jit_solution(3639337899189808997)
XLA Ops:
  0.7 0.6 compare_reduce_fusion
  1.3 0.8 dynamic-slice_convert_fusion
  2.1 0.7 pad.19.ids_ref
  2.7 0.8 copy.27
  3.6 0.6 pad.22.hin
  4.2 0.8 copy.25.labels
  5.0 0.8 copy-done.1
  5.7 17.3 %shard_map.136 = (bf16[4,2,2,2,64,128]{5,4,3,2,1,0:T(8,128)(2,1)S(1)}, s32[4,2,2,8,128]{4,3,2,1,0:T(8,128)S(1)}) custom-call(bf16[2,64,128]{2,1,0:T(8,128)(2,1)S(1)} %copy-done.1, s32[8,128]{1,0:T(8,128)S(1)} %pad.19.ids_ref), custom_call_target="tpu_custom_call" | custom-call | flops 1000000000 | bytes 626688 | tf_op jit(solution)/shard_map/pallas_call | solution.py:422
  23.0 0.7 fusion.3
  24.0 0.7 scatter.4.ident
  26.2 2.4 %add_multiply_fusion = (f32[2048,256]{1,0:T(8,128)}, bf16[2048,256]{1,0:T(8,128)(2,1)S(1)}) fusion(f32[256]{0:T(256)S(1)} %dynamic-slice_convert_fusion, bf16[2048,128]{1,0:T(8,128)(2,1)S(1)} %bitcast.20, bf16[128,4096]{1,0:T(8,128)(2,1)S(1)} %copy-done, s32[]{:T(128)S(6)} %select_n.4), kind=kOutput, calls=%fused_computation.2 | convolution fusion | flops 139460608 | bytes 3736580 | tf_op jit(solution)/shard_map/dot_general | solution.py:527
  28.6 0.8 slice-done.1
  29.4 5.6 %fusion.4 = bf16[32,256,256]{2,0,1:T(8,128)(2,1)S(1)} fusion(bf16[32,50]{1,0:T(8,128)(2,1)S(1)} %get-tuple-element.49, bf16[256,50,256]{2,0,1:T(8,128)(2,1)S(1)} %bitcast.23), kind=kOutput, calls=%fused_computation.15 | convolution fusion | flops 209715200 | bytes 10751104 | tf_op jit(solution)/shard_map/kh,dhc->kdc/dot_general | solution.py:523
  34.9 2.4 %fusion.8 = f32[32,64,256]{2,1,0:T(8,128)S(1)} fusion(bf16[32,64,256]{2,1,0:T(8,128)(2,1)S(1)} %bitcast.24, bf16[32,256,256]{2,0,1:T(8,128)(2,1)S(1)} %fusion.4), kind=kOutput, calls=%fused_computation.23 | convolution fusion | flops 268435456 | bytes 7340032 | tf_op jit(solution)/shard_map/krd,kdc->krc/dot_general | solution.py:530
  37.4 4.5 %copy.34.heads = bf16[32,256,256]{2,1,0:T(8,128)(2,1)} copy(bf16[32,256,256]{2,0,1:T(8,128)(2,1)S(1)} %fusion.4) | data formatting | bytes 8388608 | tf_op jit(solution)/shard_map/kh,dhc->kdc/dot_general | solution.py:523
  41.9 34.2 %shard_map.137 = bf16[4,2,2,2,64,256]{5,4,3,2,1,0:T(8,128)(2,1)S(1)} custom-call(f32[4,2,2,2,64,256]{5,4,3,2,1,0:T(8,128)S(1)} %bitcast.18, s32[2,64,1]{2,1,0:T(8,128)S(1)} %copy.25.labels), custom_call_target="tpu_custom_call" | custom-call | flops 1000000000 | bytes 3146240 | tf_op jit(solution)/shard_map/pallas_call | solution.py:422
  76.1 1.0 copy-done.2
  77.1 6.9 %copy.23.w = bf16[256,50,256]{2,1,0:T(8,128)(2,1)} copy(bf16[256,50,256]{2,0,1:T(8,128)(2,1)S(1)} %bitcast.23) | data formatting | bytes 13107200 | tf_op args[8]
  84.0 92.2 %shard_map.138 = (f32[16,50,256]{2,1,0:T(8,128)}, f32[128,4096]{1,0:T(8,128)}, f32[1,4096]{1,0:T(1,128)}, f32[512,128]{1,0:T(8,128)}, f32[128,128]{1,0:T(8,128)}, /*index=5*/f32[1,128]{1,0:T(1,128)}) custom-call(bf16[32,64,256]{2,1,0:T(8,128)(2,1)} %bitcast.25, bf16[32,64,256]{2,1,0:T(8,128)(2,1)} %bitcast.19, bf16[32,256,256]{2,1,0:T(8,128)(2,1)} %copy.34.heads, ...), custom_call_target="tpu_custom_call" | custom-call | flops 10000000000 | bytes 18928128 | tf_op jit(solution)/shard_map/pallas_call | solution.py:422
  176.2 1.1 slice_bitcast_fusion
  177.4 1.5 copy.29
  178.9 2.3 %copy.30 = f32[16,50,256]{2,0,1:T(8,128)} copy(f32[16,50,256]{2,1,0:T(8,128)} %get-tuple-element.45) | data formatting | bytes 1638400
  181.3 3.2 %copy.40 = f32[128,4096]{1,0:T(8,128)} copy(f32[128,4096]{1,0:T(8,128)} %get-tuple-element.56) | data formatting | bytes 4194304
  185.0 0.7 copy.42
  (29 shorter events, 2.4 us)
Async XLA Ops:
  0.6 25.6 %copy-start = (bf16[128,4096]{1,0:T(8,128)(2,1)S(1)}, bf16[128,4096]{1,0:T(8,128)(2,1)}, u32[]{:S(2)}) copy-start(bf16[128,4096]{1,0:T(8,128)(2,1)} %param.14) | copy-start | bytes 3145732
  0.6 24.0 %copy-start.7 = (bf16[128,50]{0,1:T(8,128)(2,1)S(1)}, bf16[128,50]{0,1:T(8,128)(2,1)}, u32[]{:S(2)}) copy-start(bf16[128,50]{0,1:T(8,128)(2,1)} %param.17) | copy-start | bytes 38404
  0.7 24.0 %copy-start.8 = (bf16[512,128]{1,0:T(8,128)(2,1)S(1)}, bf16[512,128]{1,0:T(8,128)(2,1)}, u32[]{:S(2)}) copy-start(bf16[512,128]{1,0:T(8,128)(2,1)} %emb.1) | copy-start | bytes 393220
  0.7 24.0 %copy-start.9 = (f32[50]{0:T(128)S(1)}, f32[50]{0:T(128)}, u32[]{:S(2)}) copy-start(f32[50]{0:T(128)} %param.18) | copy-start | bytes 604
  5.0 0.8 copy-start.1
  23.0 5.6 %copy-start.3 = (bf16[4,2,2,2,64,128]{5,4,3,2,1,0:T(8,128)(2,1)}, bf16[4,2,2,2,64,128]{5,4,3,2,1,0:T(8,128)(2,1)S(1)}, u32[]{:S(2)}) copy-start(bf16[4,2,2,2,64,128]{5,4,3,2,1,0:T(8,128)(2,1)S(1)} %get-tuple-element.26) | copy-start | bytes 1572868
  25.6 3.0 %slice-start = ((s8[6553600]{0:T(1024)(128)(4,1)}), s8[4194304]{0:T(1024)(128)(4,1)S(1)}, s32[]{:S(2)}) async-start(s8[6553600]{0:T(1024)(128)(4,1)} %bitcast.22), calls=%async_computation | async-start | bytes 8388608
  26.2 3.2 %slice-start.1 = ((s8[6553600]{0:T(1024)(128)(4,1)}), s8[2359296]{0:T(1024)(128)(4,1)S(1)}, s32[]{:S(2)}) async-start(s8[6553600]{0:T(1024)(128)(4,1)} %bitcast.22), calls=%async_computation.1 | async-start | bytes 4718592
  28.6 6.3 %copy-start.4 = (bf16[2048,256]{1,0:T(8,128)(2,1)}, bf16[2048,256]{1,0:T(8,128)(2,1)S(1)}, u32[]{:S(2)}) copy-start(bf16[2048,256]{1,0:T(8,128)(2,1)S(1)} %get-tuple-element.47) | copy-start | bytes 3145732
  76.1 1.0 copy-start.2
  181.3 3.2 %copy-start.6 = (f32[1,4096]{1,0:T(1,128)S(1)}, f32[1,4096]{1,0:T(1,128)}, u32[]{:S(2)}) copy-start(f32[1,4096]{1,0:T(1,128)} %get-tuple-element.29) | copy-start | bytes 49156
  181.3 3.8 %copy-start.5 = (f32[512,128]{1,0:T(8,128)S(1)}, f32[512,128]{1,0:T(8,128)}, u32[]{:S(2)}) copy-start(f32[512,128]{1,0:T(8,128)} %get-tuple-element.58) | copy-start | bytes 786436
